TPU v7x, 256 devices: a whole 4x4x8 slice. The times are simulated.
256 devices in a mesh: seq: 64 (over y, z, x_hi), tp: 4 (over x_lo, core).
Axes of the slice: x: 4 (x_hi: 2, x_lo: 2; x = x_hi * 2 + x_lo), y: 4, z: 8, core: 2. Of those that a mesh axis runs over, the one named last changes fastest.
Arguments:
- inputs: bfloat16 [8192, 2048], P(('seq', 'tp')), may hold values from -40 to 40
- gain: float32 [2048], replicated, may hold values from 0.5 to 1.5
- w_gate: bfloat16 [2048, 7168], P('seq', 'tp'), may hold values from -0.125 to 0.125
- w_up: bfloat16 [2048, 7168], P('seq', 'tp'), may hold values from -0.125 to 0.125
- grad_act: bfloat16 [8192, 7168], P('seq', 'tp'), may hold values from -12 to 12
Outputs:
- input_grad: bfloat16 [8192, 2048], P(('seq', 'tp'))
- gain_grad: float32 [2048], replicated
- gate_weight_grad: float32 [2048, 7168], P('seq', 'tp')
All inputs are finite; a program needn't handle non-finite values.
Results may differ from a plain program's by a relative error of at most 0.012.
Values may be sent and summed in bfloat16 or wider, within the bound.
No kernel may reach another device: no remote copies, remote signals or barrier semaphores. Data moves between devices by JAX's collectives and lax.ppermute only.
A program may use at most 128 MiB of HBM per device.

v0:
```python
import jax
import jax.numpy as jnp
from jax import lax
from jax.sharding import Mesh
from jax.sharding import PartitionSpec as P

TP = ("tp_0", "tp_1")
SEQ = ("seq_0", "seq_1", "seq_2")
SEQ_TP = ("seq_0", "seq_1", "seq_2", "tp_0", "tp_1")


def sent_to_all(value, axis):
    peers = lax.axis_size(axis)
    return lax.all_to_all(
        jnp.broadcast_to(value[None], (peers, *value.shape)), axis, 0, 0, tiled=True
    )


def laid_out(parts, dim):
    dims = list(parts.shape[1:])
    dims[dim] *= parts.shape[0]
    return jnp.moveaxis(parts, 0, dim).reshape(dims)


def collect(value, axis, dim):
    parts = sent_to_all(value, axis)
    return laid_out(parts, dim)


def in_one_piece(arrays, axis, dim, along):
    widths = [a.shape[along] for a in arrays]
    both = jnp.concatenate(arrays, axis=along)
    out = lax.all_gather(both, axis, axis=dim, tiled=True)
    return tuple(jnp.split(out, [sum(widths[:k]) for k in range(1, len(widths))], axis=along))


def split_up(value, dim, peers):
    dims = value.shape
    parts = value.reshape(*dims[:dim], peers, dims[dim] // peers, *dims[dim + 1 :])
    return jnp.moveaxis(parts, dim, 0)


def sum_at_owner(value, axis, dim):
    parts = split_up(value, dim, lax.axis_size(axis))
    arrived = lax.all_to_all(parts, axis, split_axis=0, concat_axis=0, tiled=True)
    return arrived.astype(jnp.float32).sum(axis=0)


def over_axes(value, axes):
    for axis in axes:
        value = lax.psum(value, axis)
    return value


def own_rows_2(terms, axes):
    so_far = terms.astype(jnp.bfloat16)
    for axis in axes:
        so_far = lax.psum_scatter(so_far, axis, scatter_dimension=0, tiled=True)
    return so_far.astype(jnp.float32)


def on_device(inputs, gain, w_gate, w_up, grad_act):
    group_inputs = collect(inputs, TP, 0)
    values = group_inputs.astype(jnp.float32)
    inverse = lax.rsqrt(jnp.mean(values * values, axis=-1, keepdims=True) + 1e-05)
    scaled = values * inverse
    normed = (scaled * gain).astype(jnp.bfloat16)
    full_gate, full_up = in_one_piece((w_gate, w_up), SEQ, 0, 1)
    gate = jnp.dot(normed, full_gate, preferred_element_type=jnp.float32)
    up = jnp.dot(normed, full_up, preferred_element_type=jnp.float32)
    sigmoid_gate = jax.nn.sigmoid(gate)
    cotangent = grad_act.astype(jnp.float32)
    d_up = (cotangent * gate * sigmoid_gate).astype(jnp.bfloat16)
    d_gate = (cotangent * up * sigmoid_gate * (1.0 + gate * (1.0 - sigmoid_gate))).astype(
        jnp.bfloat16
    )
    contract = (((1,), (1,)), ((), ()))
    partial_grad = lax.dot_general(d_gate, full_gate, contract, preferred_element_type=jnp.float32)
    partial_grad = partial_grad + lax.dot_general(
        d_up, full_up, contract, preferred_element_type=jnp.float32
    )
    own_grad = sum_at_owner(partial_grad.astype(jnp.bfloat16), TP, 0)
    own_rows = own_grad.shape[0]
    offset = lax.axis_index(TP) * own_rows
    own_scaled = lax.dynamic_slice_in_dim(scaled, offset, own_rows, 0)
    own_inverse = lax.dynamic_slice_in_dim(inverse, offset, own_rows, 0)
    gain_grad = over_axes(jnp.sum(own_grad * own_scaled, axis=0), SEQ_TP)
    gained = own_grad * gain
    middle = jnp.mean(gained * own_scaled, axis=-1, keepdims=True)
    input_grad = (own_inverse * (gained - own_scaled * middle)).astype(jnp.bfloat16)
    gate_weight_grad = own_rows_2(
        lax.dot_general(
            normed, d_gate, (((0,), (0,)), ((), ())), preferred_element_type=jnp.float32
        ),
        SEQ,
    )
    return (input_grad, gain_grad, gate_weight_grad)


def solution(mesh):
    torus = Mesh(mesh.devices.reshape(4, 8, 2, 2, 2), ("seq_0", "seq_1", "seq_2", "tp_0", "tp_1"))
    placed = (P(SEQ_TP, None), P(), P(SEQ, TP), P(SEQ, TP), P(SEQ, TP))
    return jax.shard_map(
        on_device,
        mesh=torus,
        in_specs=placed,
        out_specs=(P(SEQ_TP, None), P(), P(SEQ, TP)),
        check_vma=False,
    )
```

profile of v0, /device:TPU:1, one launch (start us, length us, event | category | flops | bytes accessed | tf_op | source)
XLA Modules:
  0.0 380.7 jit_solution(14655092618514983426)
XLA Ops:
  7.2 0.0 all-gather.2.cloned.1.call-start
  7.2 1.7 pad_maximum_fusion
  8.9 0.0 reduce-scatter.4.cloned.1.call-start
  9.0 1.0 broadcast_in_dim.2
  10.0 13.4 %all_to_all.10 = bf16[4,32,2048]{2,1,0:T(8,128)(2,1)S(1)} all-to-all(bf16[4,32,2048]{2,1,0:T(8,128)(2,1)S(1)} %broadcast_in_dim.2), channel_id=1, replica_groups=mesh['seq_0'=4,'seq_1'=8,'seq_2'=2,'tp_0'=2,'tp_1'=2] {'tp_0','tp_1'}, dimensions={0} | all-to-all | bytes 1048576 | tf_op jit(solution)/shard_map/all_to_all | solution.py:14
  23.3 0.2 multiply_reduce_fusion
  23.5 0.1 rsqrt.20
  23.6 0.9 bitcast_multiply_fusion
  24.5 184.2 %all-gather.2.cloned.1.call-done = bf16[2048,3584]{1,0:T(8,128)(2,1)} async-done(((bf16[32,3584]{1,0:T(8,128)(2,1)}), bf16[2048,3584]{1,0:T(8,128)(2,1)}) %all-gather.2.cloned.1.call-update) | async-done | bytes 14680080 | tf_op jit(solution)/shard_map/all_gather | solution.py:33
  208.7 4.2 %fusion.2 = f32[128,1792]{1,0:T(8,128)S(1)} fusion(bf16[128,2048]{1,0:T(8,128)(2,1)S(1)} %get-tuple-element.6, bf16[2048,3584]{1,0:T(8,128)(2,1)} %all-gather.2.cloned.1.call-done), kind=kOutput, calls=%fused_computation.3 | convolution fusion | flops 939524096 | bytes 8781824 | tf_op jit(solution)/shard_map/dot_general | solution.py:69
  212.9 4.5 %fusion.23 = bf16[128,1792]{1,0:T(8,128)(2,1)S(1)} fusion(bf16[128,2048]{1,0:T(8,128)(2,1)S(1)} %get-tuple-element.6, bf16[2048,3584]{1,0:T(8,128)(2,1)} %all-gather.2.cloned.1.call-done, bf16[128,1792]{1,0:T(8,128)(2,1)S(1)} %copy-done.1, f32[128,1792]{1,0:T(8,128)S(1)} %fusion.2), kind=kOutput, calls=%fused_computation.14 | convolution fusion | flops 942047232 | bytes 9699328 | tf_op jit(solution)/shard_map/dot_general | solution.py:70
  217.4 5.0 %convolution_convert_fusion = bf16[2048,1792]{1,0:T(8,128)(2,1)} fusion(bf16[128,2048]{1,0:T(8,128)(2,1)S(1)} %get-tuple-element.6, bf16[128,1792]{1,0:T(8,128)(2,1)S(1)} %fusion.23), kind=kOutput, calls=%fused_computation | convolution fusion | flops 943194112 | bytes 8323072 | tf_op jit(solution)/shard_map/dot_general | solution.py:92
  222.5 0.0 reduce-scatter.6.cloned.1.call-start
  222.5 72.7 %reduce-scatter.4.cloned.1.call-done = bf16[512,1792]{1,0:T(8,128)(2,1)} async-done(((bf16[2048,1792]{1,0:T(8,128)(2,1)}), bf16[512,1792]{1,0:T(8,128)(2,1)}) %reduce-scatter.4.cloned.1.call-update) | async-done | bytes 1835024 | tf_op jit(solution)/shard_map/reduce_scatter | solution.py:58
  295.3 5.5 %fusion = f32[128,2048]{1,0:T(8,128)S(1)} fusion(bf16[128,1792]{1,0:T(8,128)(2,1)S(1)} %fusion.23, bf16[2048,3584]{1,0:T(8,128)(2,1)} %all-gather.2.cloned.1.call-done), kind=kOutput, calls=%fused_computation.1 | convolution fusion | flops 939524096 | bytes 8847360 | tf_op jit(solution)/shard_map/dot_general | solution.py:78
  300.8 6.4 %fusion.20 = bf16[128,2048]{1,0:T(8,128)(2,1)} fusion(f32[128,2048]{1,0:T(8,128)S(1)} %fusion, bf16[2048,3584]{1,0:T(8,128)(2,1)} %all-gather.2.cloned.1.call-done, f32[128,1792]{1,0:T(8,128)S(1)} %fusion.2, bf16[128,1792]{1,0:T(8,128)(2,1)S(1)} %copy-done.1), kind=kOutput, calls=%fused_computation.13 | convolution fusion | flops 941654016 | bytes 10289152 | tf_op jit(solution)/shard_map/dot_general | solution.py:79
  307.2 4.2 %all-to-all-start.1 = ((bf16[4,32,2048]{2,1,0:T(8,128)(2,1)}), bf16[4,32,2048]{2,1,0:T(8,128)(2,1)S(1)}, u32[]{:S(2)}, u32[]{:S(2)}) async-start(bf16[4,32,2048]{2,1,0:T(8,128)(2,1)} %bitcast.2), calls=%async_computation.1 | async-start | bytes 1048576 | tf_op jit(solution)/shard_map/all_to_all | solution.py:45
  311.4 0.1 rsqrt.19
  311.5 0.1 dynamic-slice_bitcast_fusion
  311.5 7.7 %all-to-all-done.1 = bf16[4,32,2048]{2,1,0:T(8,128)(2,1)S(1)} async-done(((bf16[4,32,2048]{2,1,0:T(8,128)(2,1)}), bf16[4,32,2048]{2,1,0:T(8,128)(2,1)S(1)}, u32[]{:S(2)}, u32[]{:S(2)}) %all-to-all-start.1) | async-done | bytes 524320 | tf_op jit(solution)/shard_map/all_to_all | solution.py:45
  319.2 0.1 convert_reduce_fusion
  319.3 0.2 multiply_reduce_fusion.1
  319.5 7.5 %psum.35 = f32[2048]{0:T(1024)S(1)} all-reduce(f32[2048]{0:T(1024)S(1)} %get-tuple-element.3), channel_id=1, replica_groups=mesh['seq_0'=4,'seq_1'=8,'seq_2'=2,'tp_0'=2,'tp_1'=2] {'seq_0'}, use_global_device_ids=true, to_apply=%region_4.0 | all-reduce | flops 2048 | bytes 16384 | tf_op jit(solution)/shard_map/psum | solution.py:51
  327.0 13.8 %psum.36 = f32[2048]{0:T(1024)S(1)} all-reduce(f32[2048]{0:T(1024)S(1)} %psum.35), channel_id=1, replica_groups=mesh['seq_0'=4,'seq_1'=8,'seq_2'=2,'tp_0'=2,'tp_1'=2] {'seq_1'}, use_global_device_ids=true, to_apply=%region_5.0 | all-reduce | flops 2048 | bytes 16384 | tf_op jit(solution)/shard_map/psum | solution.py:51
  340.8 5.4 %psum.37 = f32[2048]{0:T(1024)S(1)} all-reduce(f32[2048]{0:T(1024)S(1)} %psum.36), channel_id=1, replica_groups=mesh['seq_0'=4,'seq_1'=8,'seq_2'=2,'tp_0'=2,'tp_1'=2] {'seq_2'}, use_global_device_ids=true, to_apply=%region_6.0 | all-reduce | flops 2048 | bytes 16384 | tf_op jit(solution)/shard_map/psum | solution.py:51
  346.2 3.8 %psum.38 = f32[2048]{0:T(1024)S(1)} all-reduce(f32[2048]{0:T(1024)S(1)} %psum.37), channel_id=1, replica_groups=mesh['seq_0'=4,'seq_1'=8,'seq_2'=2,'tp_0'=2,'tp_1'=2] {'tp_0'}, use_global_device_ids=true, to_apply=%region_7.0 | all-reduce | flops 2048 | bytes 16384 | tf_op jit(solution)/shard_map/psum | solution.py:51
  350.0 0.0 reduce-scatter.6.cloned.1.call-done
  350.1 0.0 reduce-scatter.8.cloned.1.call-update
  350.1 11.1 %psum.39 = f32[2048]{0:T(1024)} all-reduce(f32[2048]{0:T(1024)S(1)} %psum.38), channel_id=1, replica_groups=mesh['seq_0'=4,'seq_1'=8,'seq_2'=2,'tp_0'=2,'tp_1'=2] {'tp_1'}, use_global_device_ids=true, to_apply=%region_8.0 | all-reduce | flops 2048 | bytes 16384 | tf_op jit(solution)/shard_map/psum | solution.py:51
  361.1 0.8 multiply_convert_fusion.1
  361.9 10.7 %reduce-scatter.8.cloned.1.call-done = bf16[32,1792]{1,0:T(8,128)(2,1)} async-done(((bf16[64,1792]{1,0:T(8,128)(2,1)}), bf16[32,1792]{1,0:T(8,128)(2,1)}) %reduce-scatter.8.cloned.1.call-update) | async-done | bytes 114704 | tf_op jit(solution)/shard_map/reduce_scatter | solution.py:58
  372.6 1.6 convert_element_type.47
  (10 shorter events, 0.1 us)
Async XLA Ops:
  7.2 201.5 %all-gather.2.cloned.1.call-start = ((), (), s32[]{:S(2)}) async-start(), calls=%async_computation.5 | async-start | bytes 14909440 | tf_op jit(solution)/shard_map/all_gather | solution.py:33
  8.9 204.0 %copy-start.1 = (bf16[128,1792]{1,0:T(8,128)(2,1)S(1)}, bf16[128,1792]{1,0:T(8,128)(2,1)}, u32[]{:S(2)}) copy-start(bf16[128,1792]{1,0:T(8,128)(2,1)} %param.9) | copy-start | bytes 1376260
  8.9 286.3 %reduce-scatter.4.cloned.1.call-start = ((), (), s32[]{:S(2)}) async-start(), calls=%async_computation.6 | async-start | bytes 9175040 | tf_op jit(solution)/shard_map/reduce_scatter | solution.py:58
  222.5 127.6 %reduce-scatter.6.cloned.1.call-start = ((), (), s32[]{:S(2)}) async-start(), calls=%async_computation.7 | async-start | bytes 2064384 | tf_op jit(solution)/shard_map/reduce_scatter | solution.py:58
  300.8 18.5 %copy-start = (f32[2048]{0:T(1024)S(1)}, f32[2048]{0:T(1024)}, u32[]{:S(2)}) copy-start(f32[2048]{0:T(1024)} %param.6) | copy-start | bytes 24580
  307.2 12.0 %all-to-all-start.1 = ((bf16[4,32,2048]{2,1,0:T(8,128)(2,1)}), bf16[4,32,2048]{2,1,0:T(8,128)(2,1)S(1)}, u32[]{:S(2)}, u32[]{:S(2)}) async-start(bf16[4,32,2048]{2,1,0:T(8,128)(2,1)} %bitcast.2), calls=%async_computation.1 | async-start | bytes 1048576 | tf_op jit(solution)/shard_map/all_to_all | solution.py:45
  311.4 61.2 %reduce-scatter.8.cloned.1.call-start = ((), (), s32[]{:S(2)}) async-start(), calls=%async_computation.8 | async-start | bytes 344064 | tf_op jit(solution)/shard_map/reduce_scatter | solution.py:58
Sparse Core Ops, SparseCore 0:
  12.2 196.4 all-gather.1
  222.6 72.5 reduce-scatter.3
  297.8 37.3 reduce-scatter.5
  350.2 22.3 reduce-scatter.7
where the time goes:
time: 381 us
  waiting for transfers between devices  275 us (72%)
  blocking collectives  55 us (14%)
  matrix products  25.7 us (7%)
  between operations  13.9 us (4%)
  other arithmetic  5.36 us (1%)
  starting transfers between devices  4.29 us (1%)
    all_gather x1, waiting for transfers between devices, in_one_piece(): out = lax.all_gather(both, axis, axis=dim, tiled=True)  184 us
    reduce_scatter x3, waiting for transfers between devices, own_rows_2(): so_far = lax.psum_scatter(so_far, axis, scatter_dimension=0, tiled=True)  83.4 us
    psum x5, blocking collectives, over_axes(): value = lax.psum(value, axis)  41.6 us
    all_to_all x1, blocking collectives, sent_to_all(): lax.all_to_all(jnp.broadcast_to(value[None], (peers, *value.shape)), axis...  13.4 us
    all_to_all x1, waiting for transfers between devices, sum_at_owner(): lax.all_to_all(parts, axis, split_axis=0, concat_axis=0, tiled=True)  7.69 us
  transfers between devices with their start and end apart: 5, of which 4 were waited for; matrix products, arithmetic and copies ran while one was open for 4% of the time, Pallas kernels for 0%

commit v1 on v0

v1 whole, which is shorter than its diff:
```python
import jax
import jax.numpy as jnp
from jax import lax
from jax.sharding import Mesh
from jax.sharding import PartitionSpec as P

SHAPE = (4, 2, 2, 2, 2, 2, 2)
AXES = ("y", "z1", "z0", "zv", "xh", "xl", "c")
TP = ("xl", "c")
SEQ = ("y", "z1", "z0", "zv", "xh")
SEQ_TP = SEQ + TP
Z = ("z1", "z0", "zv")
PLANE = ("y", "xl", "xh")
SWAPPED = ("z1", "z0", "zv", "xh", "xl", "c")
HALF = 896


def index_of(bits):
    value = 0
    for bit in bits:
        value = value * 2 + bit
    return value


def all_bits():
    for k in range(64):
        yield tuple((k >> (5 - j)) & 1 for j in range(6))


def piece_pairs(m):
    pairs = []
    for z1, z0, zv, xh, xl, c in all_bits():
        there = (xl, c, xh ^ m, zv, z1, z0)
        pairs.append((index_of((z1, z0, zv, xh, xl, c)), index_of(there)))
    return pairs


def row_pairs():
    pairs = []
    for z1, z0, zv, xh, xl, c in all_bits():
        there = (xh, xl, c, zv, z1, z0)
        pairs.append((index_of((z1, z0, zv, xh, xl, c)), index_of(there)))
    return pairs


def back(pairs):
    return [(b, a) for a, b in pairs]


def move(value, pairs):
    return lax.ppermute(value, SWAPPED, pairs)


def to_peer(value):
    return lax.ppermute(value, "c", [(0, 1), (1, 0)])


def in_order(first, second, flag):
    return jnp.where(flag, second, first), jnp.where(flag, first, second)


def sent_to_all(value, axes):
    peers = lax.axis_size(axes)
    return lax.all_to_all(
        jnp.broadcast_to(value[None], (peers, *value.shape)), axes, 0, 0, tiled=True
    )


def tiles_of(value, parity):
    return jnp.concatenate(
        [value[..., 128 * k : 128 * (k + 1)] for k in range(parity, 16, 2)], axis=-1
    )


def own_first(value, core):
    even, odd = tiles_of(value, 0), tiles_of(value, 1)
    return jnp.concatenate(in_order(even, odd, core), axis=-1)


def as_stored(value, core):
    even, odd = in_order(value[..., :1024], value[..., 1024:], core)
    parts = []
    for k in range(8):
        parts.append(even[..., 128 * k : 128 * (k + 1)])
        parts.append(odd[..., 128 * k : 128 * (k + 1)])
    return jnp.concatenate(parts, axis=-1)


def on_device(inputs, gain, w_gate, w_up, grad_act):
    core = lax.axis_index("c") == 1
    low = lax.axis_index("zv") == 1
    high = lax.axis_index("xh") == 1

    both = jnp.concatenate((w_gate, w_up), axis=0)
    sent = in_order(both[:, :HALF], both[:, HALF:], high)
    got = [move(sent[m], piece_pairs(m)) for m in range(2)]
    own_inputs = move(inputs, row_pairs())
    sent = in_order(grad_act[:, :HALF], grad_act[:, HALF:], high)
    got_act = [move(sent[m], piece_pairs(m)) for m in range(2)]

    first, second = in_order(got[0], got[1], low)
    gate_piece = jnp.concatenate((first[:32], second[:32]), axis=0)
    up_piece = jnp.concatenate((first[32:], second[32:]), axis=0)
    gate_own = sent_to_all(gate_piece, PLANE).reshape(1024, HALF)
    up_own = sent_to_all(up_piece, PLANE).reshape(1024, HALF)
    gate_peer = to_peer(gate_own)
    up_peer = to_peer(up_own)

    own_inputs = own_first(own_inputs, core)
    gain_here = own_first(gain, core)
    values = sent_to_all(own_inputs, Z).reshape(256, 2048).astype(jnp.float32)
    inverse = lax.rsqrt(jnp.mean(values * values, axis=-1, keepdims=True) + 1e-05)
    scaled = values * inverse
    normed = (scaled * gain_here).astype(jnp.bfloat16)
    normed_own, normed_peer = normed[:, :1024], normed[:, 1024:]

    def product(own, peer):
        return jnp.dot(normed_own, own, preferred_element_type=jnp.float32) + jnp.dot(
            normed_peer, peer, preferred_element_type=jnp.float32
        )

    gate = product(gate_own, gate_peer)
    up = product(up_own, up_peer)
    sigmoid_gate = jax.nn.sigmoid(gate)
    cotangent = jnp.concatenate(in_order(got_act[0], got_act[1], low), axis=0).astype(jnp.float32)
    d_up = (cotangent * gate * sigmoid_gate).astype(jnp.bfloat16)
    d_gate = (cotangent * up * sigmoid_gate * (1.0 + gate * (1.0 - sigmoid_gate))).astype(
        jnp.bfloat16
    )

    over_tokens = (((0,), (0,)), ((), ()))
    for_peer = lax.dot_general(
        normed_peer, d_gate, over_tokens, preferred_element_type=jnp.float32
    ).astype(jnp.bfloat16)
    from_peer = to_peer(for_peer)
    for_own = lax.dot_general(normed_own, d_gate, over_tokens, preferred_element_type=jnp.float32)
    chip_grad = (for_own + from_peer.astype(jnp.float32)).astype(jnp.bfloat16)
    arrived = lax.all_to_all(chip_grad.reshape(16, 64, HALF), PLANE, 0, 0, tiled=True)
    rows = arrived.astype(jnp.float32).sum(axis=0).astype(jnp.bfloat16)

    contract = (((1,), (1,)), ((), ()))

    def partial(gate_part, up_part):
        return lax.dot_general(
            d_gate, gate_part, contract, preferred_element_type=jnp.float32
        ) + lax.dot_general(d_up, up_part, contract, preferred_element_type=jnp.float32)

    partial_grad = jnp.concatenate(
        (partial(gate_own, up_own), partial(gate_peer, up_peer)), axis=1
    )
    parts = lax.all_to_all(
        partial_grad.astype(jnp.bfloat16).reshape(8, 32, 2048), Z, 0, 0, tiled=True
    )
    terms = as_stored(jnp.sum(partial_grad * scaled, axis=0), core)
    terms = sent_to_all(terms, ("z1", "z0", "zv", "c")).sum(axis=0)
    gain_grad = sent_to_all(terms, PLANE).sum(axis=0)

    own_grad = parts.astype(jnp.float32).sum(axis=0)
    own_values = own_inputs.astype(jnp.float32)
    own_inverse = lax.rsqrt(jnp.mean(own_values * own_values, axis=-1, keepdims=True) + 1e-05)
    own_scaled = own_values * own_inverse
    gained = own_grad * gain_here
    middle = jnp.mean(gained * own_scaled, axis=-1, keepdims=True)
    own_input_grad = (own_inverse * (gained - own_scaled * middle)).astype(jnp.bfloat16)
    input_grad = move(as_stored(own_input_grad, core), back(row_pairs()))

    sent = in_order(rows[:32], rows[32:], low)
    got = [move(sent[m], back(piece_pairs(m))) for m in range(2)]
    gate_weight_grad = jnp.concatenate(in_order(got[0], got[1], high), axis=1).astype(jnp.float32)
    return (input_grad, gain_grad, gate_weight_grad)


def solution(mesh):
    torus = Mesh(mesh.devices.reshape(SHAPE), AXES)
    placed = (P(SEQ_TP, None), P(), P(SEQ, TP), P(SEQ, TP), P(SEQ, TP))
    return jax.shard_map(
        on_device,
        mesh=torus,
        in_specs=placed,
        out_specs=(P(SEQ_TP, None), P(), P(SEQ, TP)),
        check_vma=False,
    )
```

time: 381 us -> 255 us (0.67)
  waiting for transfers between devices: 275 us -> 140 us
  starting transfers between devices: 4.29 us -> 73.6 us
  blocking collectives: 55 us -> 0 us
  between operations: 13.9 us -> 1.36 us
  local copies, waits for them, and re-layouts: 1.25 us -> 10.1 us
  matrix products: 25.7 us -> 17.9 us
    all_gather x1 -> x0, waiting for transfers between devices: 184 us -> none  [in_one_piece(): out = lax.all_gather(both, axis, axis=dim, tiled=True)]
    all_to_all x1 -> x7, waiting for transfers between devices: 7.69 us -> 131 us  [the longest x5 80.9 us: sent_to_all(): lax.all_to_all(jnp.broadcast_to(value[None], (peers, *value.shape)), axes...]
    reduce_scatter x3 -> x0, waiting for transfers between devices: 83.4 us -> none  [own_rows_2(): so_far = lax.psum_scatter(so_far, axis, scatter_dimension=0, tiled=True)]
    psum x5 -> x0, blocking collectives: 41.6 us -> none  [over_axes(): value = lax.psum(value, axis)]
    all_to_all x1 -> x7, starting transfers between devices: 4.16 us -> 45.1 us  [the longest x5 36 us: sent_to_all(): lax.all_to_all(jnp.broadcast_to(value[None], (peers, *value.shape)), axes...]
    ppermute x0 -> x11, starting transfers between devices: none -> 28.6 us  [the longest x8 27.3 us: move(): return lax.ppermute(value, SWAPPED, pairs)]
    all_to_all x1 -> x0, blocking collectives: 13.4 us -> none  [sent_to_all(): lax.all_to_all(jnp.broadcast_to(value[None], (peers, *value.shape)), axis...]
    ppermute x0 -> x11, waiting for transfers between devices: none -> 8.35 us  [the longest x8 8.34 us: move(): return lax.ppermute(value, SWAPPED, pairs)]
  transfers between devices with their start and end apart: 5 -> 18, of which waited for: 4 -> 9; matrix products, arithmetic and copies ran while one was open for 4% -> 7% of each run, Pallas kernels for 0% -> 0%
where the time goes in v1:
time: 255 us; the launch traced here: 251 us
  waiting for transfers between devices  140 us (55%)
  starting transfers between devices  73.6 us (29%)
  matrix products  17.9 us (7%)
  local copies, waits for them, and re-layouts  10.1 us (4%)
  other arithmetic  8.42 us (3%)
    all_to_all x5, waiting for transfers between devices, sent_to_all(): lax.all_to_all(jnp.broadcast_to(value[None], (peers, *value.shape)), axes...  80.9 us
    all_to_all x5, starting transfers between devices, sent_to_all(): lax.all_to_all(jnp.broadcast_to(value[None], (peers, *value.shape)), axes...  36 us
    ppermute x8, starting transfers between devices, move(): return lax.ppermute(value, SWAPPED, pairs)  27.3 us
    all_to_all x1, waiting for transfers between devices, on_device(): lax.all_to_all(partial_grad.astype(jnp.bfloat16).reshape(8, 32, 2048), Z,...  27.1 us
    all_to_all x1, waiting for transfers between devices, on_device(): lax.all_to_all(chip_grad.reshape(16, 64, HALF), PLANE, 0, 0, tiled=True)  23.2 us
    ppermute x8, waiting for transfers between devices, move(): return lax.ppermute(value, SWAPPED, pairs)  8.34 us
    broadcast_in_dim x5, local copies, waits for them, and re-layouts, sent_to_all(): jnp.broadcast_to(value[None], (peers, *value.shape))  5.69 us
    all_to_all x1, starting transfers between devices, on_device(): lax.all_to_all(chip_grad.reshape(16, 64, HALF), PLANE, 0, 0, tiled=True)  5.46 us
  transfers between devices with their start and end apart: 18, of which 9 were waited for; matrix products, arithmetic and copies ran while one was open for 7% of the time, Pallas kernels for 0%

profile of v1, /device:TPU:1, one launch (start us, length us, event | category | flops | bytes accessed | tf_op | source)
XLA Modules:
  0.0 250.9 jit_solution(11123488814518381804)
XLA Ops:
  2.5 5.8 %collective-permute-start.3 = (bf16[64,896]{1,0:T(8,128)(2,1)S(1)}, bf16[64,896]{1,0:T(8,128)(2,1)S(1)}, u32[]{:S(2)}, u32[]{:S(2)}) collective-permute-start(bf16[64,896]{1,0:T(8,128)(2,1)S(1)} %get-tuple-element.9), channel_id=1, source_target_pairs={{0,8},{1,24},{2,40},{3,56},{4,0},{5,16},{6,32},{7,48},{8,12},{9,28... | collective-permute-start | bytes 344072 | tf_op jit(solution)/shard_map/ppermute | solution.py:51
  8.3 1.9 collective-permute-start.4
  10.2 1.8 collective-permute-done.3
  12.0 3.5 %collective-permute-done.4 = bf16[64,896]{1,0:T(8,128)(2,1)S(1)} collective-permute-done((bf16[64,896]{1,0:T(8,128)(2,1)S(1)}, bf16[64,896]{1,0:T(8,128)(2,1)S(1)}, u32[]{:S(2)}, u32[]{:S(2)}) %collective-permute-start.4) | collective-permute-done | bytes 114720 | tf_op jit(solution)/shard_map/ppermute | solution.py:51
  17.1 15.8 %all-to-all-start.1 = ((bf16[16,64,896]{2,1,0:T(8,128)(2,1)}), bf16[16,64,896]{2,1,0:T(8,128)(2,1)S(1)}, u32[]{:S(2)}, u32[]{:S(2)}) async-start(bf16[16,64,896]{2,1,0:T(8,128)(2,1)} %broadcast_in_dim.11), calls=%async_computation.1 | async-start | bytes 3670016 | tf_op jit(solution)/shard_map/all_to_all | solution.py:64
  32.8 2.9 %collective-permute-start = (bf16[32,2048]{1,0:T(8,128)(2,1)S(1)}, bf16[32,2048]{1,0:T(8,128)(2,1)S(1)}, u32[]{:S(2)}, u32[]{:S(2)}) collective-permute-start(bf16[32,2048]{1,0:T(8,128)(2,1)S(1)} %copy-done.9), channel_id=1, source_target_pairs={{0,0},{1,8},{2,16},{3,24},{4,32},{5,40},{6,48},{7,56},{8,4},{9,12}... | collective-permute-start | bytes 393224 | tf_op jit(solution)/shard_map/ppermute | solution.py:51
  36.6 5.1 %collective-permute-start.1 = (bf16[128,896]{1,0:T(8,128)(2,1)}, bf16[128,896]{1,0:T(8,128)(2,1)S(1)}, u32[]{:S(2)}, u32[]{:S(2)}) collective-permute-start(bf16[128,896]{1,0:T(8,128)(2,1)} %get-tuple-element.5), channel_id=1, source_target_pairs={{0,8},{1,24},{2,40},{3,56},{4,0},{5,16},{6,32},{7,48},{8,12},{9,28... | collective-permute-start | bytes 688136 | tf_op jit(solution)/shard_map/ppermute | solution.py:51
  41.7 1.9 collective-permute-start.2
  43.8 24.2 %all-to-all-done.1 = bf16[16,64,896]{2,1,0:T(8,128)(2,1)S(1)} async-done(((bf16[16,64,896]{2,1,0:T(8,128)(2,1)}), bf16[16,64,896]{2,1,0:T(8,128)(2,1)S(1)}, u32[]{:S(2)}, u32[]{:S(2)}) %all-to-all-start.1) | async-done | bytes 1835040 | tf_op jit(solution)/shard_map/all_to_all | solution.py:64
  69.8 6.4 %all-to-all-start.2 = ((bf16[16,64,896]{2,1,0:T(8,128)(2,1)}), bf16[16,64,896]{2,1,0:T(8,128)(2,1)S(1)}, u32[]{:S(2)}, u32[]{:S(2)}) async-start(bf16[16,64,896]{2,1,0:T(8,128)(2,1)} %broadcast_in_dim.12), calls=%async_computation.2 | async-start | bytes 3670016 | tf_op jit(solution)/shard_map/all_to_all | solution.py:64
  76.4 23.8 %all-to-all-done.2 = bf16[16,64,896]{2,1,0:T(8,128)(2,1)S(1)} async-done(((bf16[16,64,896]{2,1,0:T(8,128)(2,1)}), bf16[16,64,896]{2,1,0:T(8,128)(2,1)S(1)}, u32[]{:S(2)}, u32[]{:S(2)}) %all-to-all-start.2) | async-done | bytes 1835040 | tf_op jit(solution)/shard_map/all_to_all | solution.py:64
  101.2 3.8 %all-to-all-start = ((bf16[8,32,2048]{2,1,0:T(8,128)(2,1)}), bf16[8,32,2048]{2,1,0:T(8,128)(2,1)S(1)}, u32[]{:S(2)}, u32[]{:S(2)}) async-start(bf16[8,32,2048]{2,1,0:T(8,128)(2,1)} %broadcast_in_dim.10), calls=%async_computation | async-start | bytes 2097152 | tf_op jit(solution)/shard_map/all_to_all | solution.py:64
  106.4 1.8 broadcast_select_fusion.3
  108.2 26.1 %all-to-all-done = bf16[8,32,2048]{2,1,0:T(8,128)(2,1)S(1)} async-done(((bf16[8,32,2048]{2,1,0:T(8,128)(2,1)}), bf16[8,32,2048]{2,1,0:T(8,128)(2,1)S(1)}, u32[]{:S(2)}, u32[]{:S(2)}) %all-to-all-start) | async-done | bytes 1048608 | tf_op jit(solution)/shard_map/all_to_all | solution.py:64
  137.6 2.3 convolution_add_fusion.2
  140.0 2.4 fusion.6
  143.9 2.6 %fusion.27 = f32[256,1024]{1,0:T(8,128)S(1)} fusion(bf16[1024,896]{1,0:T(8,128)(2,1)} %collective-permute-done.5, f32[256,896]{1,0:T(8,128)S(1)} %convolution_add_fusion.2, bf16[128,896]{1,0:T(8,128)(2,1)S(1)} %copy-done.7, bf16[128,896]{1,0:T(8,128)(2,1)S(1)} %copy-done.6), kind=kOutput, calls=%fused_computation.135 | convolution fusion | flops 472055808 | bytes 4259840 | tf_op jit(solution)/shard_map/dot_general | solution.py:146
  146.5 2.2 convolution_add_fusion
  150.1 3.8 %all-to-all-start.4 = ((f32[16,1,2048]{2,1,0:T(1,128)}), f32[16,1,2048]{2,1,0:T(1,128)S(1)}, u32[]{:S(2)}, u32[]{:S(2)}) async-start(f32[16,1,2048]{2,1,0:T(1,128)} %broadcast_in_dim.13), calls=%async_computation.4 | async-start | bytes 262144 | tf_op jit(solution)/shard_map/all_to_all | solution.py:64
  153.9 2.3 fusion.2
  156.2 6.8 %all-to-all-done.4 = f32[16,1,2048]{2,1,0:T(1,128)S(1)} async-done(((f32[16,1,2048]{2,1,0:T(1,128)}), f32[16,1,2048]{2,1,0:T(1,128)S(1)}, u32[]{:S(2)}, u32[]{:S(2)}) %all-to-all-start.4) | async-done | bytes 131104 | tf_op jit(solution)/shard_map/all_to_all | solution.py:64
  163.1 3.6 %all-to-all-start.3 = ((bf16[8,32,2048]{2,1,0:T(8,128)(2,1)}), bf16[8,32,2048]{2,1,0:T(8,128)(2,1)S(1)}, u32[]{:S(2)}, u32[]{:S(2)}) async-start(bf16[8,32,2048]{2,1,0:T(8,128)(2,1)} %fusion.2), calls=%async_computation.3 | async-start | bytes 2097152 | tf_op jit(solution)/shard_map/all_to_all | solution.py:151
  166.8 2.0 convolution_convert_fusion
  168.9 27.1 %all-to-all-done.3 = bf16[8,32,2048]{2,1,0:T(8,128)(2,1)S(1)} async-done(((bf16[8,32,2048]{2,1,0:T(8,128)(2,1)}), bf16[8,32,2048]{2,1,0:T(8,128)(2,1)S(1)}, u32[]{:S(2)}, u32[]{:S(2)}) %all-to-all-start.3) | async-done | bytes 1048608 | tf_op jit(solution)/shard_map/all_to_all | solution.py:151
  196.6 3.5 %add_convert_fusion = bf16[1024,896]{1,0:T(8,128)(2,1)} fusion(bf16[1024,896]{1,0:T(8,128)(2,1)} %collective-permute-done.8, bf16[256,896]{1,0:T(8,128)(2,1)S(1)} %fusion.6, bf16[256,2048]{1,0:T(8,128)(2,1)S(1)} %copy-done.1), kind=kOutput, calls=%fused_computation | convolution fusion | flops 472514560 | bytes 4653056 | tf_op jit(solution)/shard_map/dot_general | solution.py:136
  200.0 5.5 %all-to-all-start.6 = ((bf16[16,64,896]{2,1,0:T(8,128)(2,1)}), bf16[16,64,896]{2,1,0:T(8,128)(2,1)S(1)}, u32[]{:S(2)}, u32[]{:S(2)}) async-start(bf16[16,64,896]{2,1,0:T(8,128)(2,1)} %bitcast.31), calls=%async_computation.6 | async-start | bytes 3670016 | tf_op jit(solution)/shard_map/all_to_all | solution.py:138
  205.6 2.5 collective-permute-start.7
  208.1 23.2 %all-to-all-done.6 = bf16[16,64,896]{2,1,0:T(8,128)(2,1)S(1)} async-done(((bf16[16,64,896]{2,1,0:T(8,128)(2,1)}), bf16[16,64,896]{2,1,0:T(8,128)(2,1)S(1)}, u32[]{:S(2)}, u32[]{:S(2)}) %all-to-all-start.6) | async-done | bytes 1835040 | tf_op jit(solution)/shard_map/all_to_all | solution.py:138
  232.1 6.2 %all-to-all-start.5 = ((f32[16,1,2048]{2,1,0:T(1,128)}), f32[16,1,2048]{2,1,0:T(1,128)S(1)}, u32[]{:S(2)}, u32[]{:S(2)}) async-start(f32[16,1,2048]{2,1,0:T(1,128)} %broadcast_in_dim.14), calls=%async_computation.5 | async-start | bytes 262144 | tf_op jit(solution)/shard_map/all_to_all | solution.py:64
  238.6 4.5 %collective-permute-start.9 = (bf16[32,896]{1,0:T(8,128)(2,1)S(1)}, bf16[32,896]{1,0:T(8,128)(2,1)S(1)}, u32[]{:S(2)}, u32[]{:S(2)}) collective-permute-start(bf16[32,896]{1,0:T(8,128)(2,1)S(1)} %get-tuple-element.33), channel_id=1, source_target_pairs={{8,0},{24,1},{40,2},{56,3},{0,4},{16,5},{32,6},{48,7},{12,8},{28,9... | collective-permute-start | bytes 172040 | tf_op jit(solution)/shard_map/ppermute | solution.py:51
  243.1 2.7 %collective-permute-start.10 = (bf16[32,896]{1,0:T(8,128)(2,1)S(1)}, bf16[32,896]{1,0:T(8,128)(2,1)S(1)}, u32[]{:S(2)}, u32[]{:S(2)}) collective-permute-start(bf16[32,896]{1,0:T(8,128)(2,1)S(1)} %get-tuple-element.34), channel_id=1, source_target_pairs={{0,0},{16,1},{32,2},{48,3},{8,4},{24,5},{40,6},{56,7},{4,8},{20,9}... | collective-permute-start | bytes 172040 | tf_op jit(solution)/shard_map/ppermute | solution.py:51
  246.5 3.1 %collective-permute-done.10 = bf16[32,896]{1,0:T(8,128)(2,1)S(1)} collective-permute-done((bf16[32,896]{1,0:T(8,128)(2,1)S(1)}, bf16[32,896]{1,0:T(8,128)(2,1)S(1)}, u32[]{:S(2)}, u32[]{:S(2)}) %collective-permute-start.10) | collective-permute-done | bytes 57376 | tf_op jit(solution)/shard_map/ppermute | solution.py:51
  (126 shorter events, 18.6 us)
Async XLA Ops:
  2.5 9.5 %collective-permute-start.3 = (bf16[64,896]{1,0:T(8,128)(2,1)S(1)}, bf16[64,896]{1,0:T(8,128)(2,1)S(1)}, u32[]{:S(2)}, u32[]{:S(2)}) collective-permute-start(bf16[64,896]{1,0:T(8,128)(2,1)S(1)} %get-tuple-element.9), channel_id=1, source_target_pairs={{0,8},{1,24},{2,40},{3,56},{4,0},{5,16},{6,32},{7,48},{8,12},{9,28... | collective-permute-start | bytes 344072 | tf_op jit(solution)/shard_map/ppermute | solution.py:51
  8.3 7.2 %collective-permute-start.4 = (bf16[64,896]{1,0:T(8,128)(2,1)S(1)}, bf16[64,896]{1,0:T(8,128)(2,1)S(1)}, u32[]{:S(2)}, u32[]{:S(2)}) collective-permute-start(bf16[64,896]{1,0:T(8,128)(2,1)S(1)} %get-tuple-element.10), channel_id=1, source_target_pairs={{0,0},{1,16},{2,32},{3,48},{4,8},{5,24},{6,40},{7,56},{8,4},{9,20}... | collective-permute-start | bytes 344072 | tf_op jit(solution)/shard_map/ppermute | solution.py:51
  17.1 15.8 %copy-start.9 = (bf16[32,2048]{1,0:T(8,128)(2,1)S(1)}, bf16[32,2048]{1,0:T(8,128)(2,1)}, u32[]{:S(2)}) copy-start(bf16[32,2048]{1,0:T(8,128)(2,1)} %param.5) | copy-start | bytes 393220
  17.1 18.7 %copy-start.5 = (bf16[128,1792]{1,0:T(8,128)(2,1)S(1)}, bf16[128,1792]{1,0:T(8,128)(2,1)}, u32[]{:S(2)}) copy-start(bf16[128,1792]{1,0:T(8,128)(2,1)} %param.9) | copy-start | bytes 1376260
  17.1 26.6 %copy-start.8 = (f32[2048]{0:T(1024)S(1)}, f32[2048]{0:T(1024)}, u32[]{:S(2)}) copy-start(f32[2048]{0:T(1024)} %param.6) | copy-start | bytes 24580
  17.1 50.9 %all-to-all-start.1 = ((bf16[16,64,896]{2,1,0:T(8,128)(2,1)}), bf16[16,64,896]{2,1,0:T(8,128)(2,1)S(1)}, u32[]{:S(2)}, u32[]{:S(2)}) async-start(bf16[16,64,896]{2,1,0:T(8,128)(2,1)} %broadcast_in_dim.11), calls=%async_computation.1 | async-start | bytes 3670016 | tf_op jit(solution)/shard_map/all_to_all | solution.py:64
  32.8 10.9 %collective-permute-start = (bf16[32,2048]{1,0:T(8,128)(2,1)S(1)}, bf16[32,2048]{1,0:T(8,128)(2,1)S(1)}, u32[]{:S(2)}, u32[]{:S(2)}) collective-permute-start(bf16[32,2048]{1,0:T(8,128)(2,1)S(1)} %copy-done.9), channel_id=1, source_target_pairs={{0,0},{1,8},{2,16},{3,24},{4,32},{5,40},{6,48},{7,56},{8,4},{9,12}... | collective-permute-start | bytes 393224 | tf_op jit(solution)/shard_map/ppermute | solution.py:51
  36.6 69.8 %collective-permute-start.1 = (bf16[128,896]{1,0:T(8,128)(2,1)}, bf16[128,896]{1,0:T(8,128)(2,1)S(1)}, u32[]{:S(2)}, u32[]{:S(2)}) collective-permute-start(bf16[128,896]{1,0:T(8,128)(2,1)} %get-tuple-element.5), channel_id=1, source_target_pairs={{0,8},{1,24},{2,40},{3,56},{4,0},{5,16},{6,32},{7,48},{8,12},{9,28... | collective-permute-start | bytes 688136 | tf_op jit(solution)/shard_map/ppermute | solution.py:51
  41.7 64.6 %collective-permute-start.2 = (bf16[128,896]{1,0:T(8,128)(2,1)}, bf16[128,896]{1,0:T(8,128)(2,1)}, u32[]{:S(2)}, u32[]{:S(2)}) collective-permute-start(bf16[128,896]{1,0:T(8,128)(2,1)} %get-tuple-element.6), channel_id=1, source_target_pairs={{0,0},{1,16},{2,32},{3,48},{4,8},{5,24},{6,40},{7,56},{8,4},{9,20}... | collective-permute-start | bytes 688136 | tf_op jit(solution)/shard_map/ppermute | solution.py:51
  68.0 1.8 copy-start.2
  69.8 30.4 %all-to-all-start.2 = ((bf16[16,64,896]{2,1,0:T(8,128)(2,1)}), bf16[16,64,896]{2,1,0:T(8,128)(2,1)S(1)}, u32[]{:S(2)}, u32[]{:S(2)}) async-start(bf16[16,64,896]{2,1,0:T(8,128)(2,1)} %broadcast_in_dim.12), calls=%async_computation.2 | async-start | bytes 3670016 | tf_op jit(solution)/shard_map/all_to_all | solution.py:64
  101.2 33.0 %all-to-all-start = ((bf16[8,32,2048]{2,1,0:T(8,128)(2,1)}), bf16[8,32,2048]{2,1,0:T(8,128)(2,1)S(1)}, u32[]{:S(2)}, u32[]{:S(2)}) async-start(bf16[8,32,2048]{2,1,0:T(8,128)(2,1)} %broadcast_in_dim.10), calls=%async_computation | async-start | bytes 2097152 | tf_op jit(solution)/shard_map/all_to_all | solution.py:64
  105.2 32.5 %collective-permute-start.6 = (bf16[1024,896]{1,0:T(8,128)(2,1)S(1)}, bf16[1024,896]{1,0:T(8,128)(2,1)}, u32[]{:S(2)}, u32[]{:S(2)}) collective-permute-start(bf16[1024,896]{1,0:T(8,128)(2,1)S(1)} %bitcast.23), channel_id=1, source_target_pairs={{0,1},{1,0},{2,3},{3,2},{4,5},{5,4},{6,7},{7,6},{8,9},{9,8},{10,11... | collective-permute-start | bytes 5505032 | tf_op jit(solution)/shard_map/ppermute | solution.py:55
  108.1 31.8 %collective-permute-start.5 = (bf16[1024,896]{1,0:T(8,128)(2,1)}, bf16[1024,896]{1,0:T(8,128)(2,1)}, u32[]{:S(2)}, u32[]{:S(2)}) collective-permute-start(bf16[1024,896]{1,0:T(8,128)(2,1)} %bitcast.28), channel_id=1, source_target_pairs={{0,1},{1,0},{2,3},{3,2},{4,5},{5,4},{6,7},{7,6},{8,9},{9,8},{10,11... | collective-permute-start | bytes 5505032 | tf_op jit(solution)/shard_map/ppermute | solution.py:55
  134.6 1.5 copy-start.3
  136.2 3.8 %copy-start = (bf16[256,2048]{1,0:T(8,128)(2,1)}, bf16[256,2048]{1,0:T(8,128)(2,1)S(1)}, u32[]{:S(2)}) copy-start(bf16[256,2048]{1,0:T(8,128)(2,1)S(1)} %fusion.1) | copy-start | bytes 3145732
  137.6 2.3 copy-start.6
  137.6 2.3 copy-start.7
  143.8 4.9 %copy-start.4 = (f32[256,1024]{1,0:T(8,128)}, f32[256,1024]{1,0:T(8,128)S(1)}, u32[]{:S(2)}) copy-start(f32[256,1024]{1,0:T(8,128)S(1)} %convolution_add_fusion.1) | copy-start | bytes 3145732
  150.1 13.0 %all-to-all-start.4 = ((f32[16,1,2048]{2,1,0:T(1,128)}), f32[16,1,2048]{2,1,0:T(1,128)S(1)}, u32[]{:S(2)}, u32[]{:S(2)}) async-start(f32[16,1,2048]{2,1,0:T(1,128)} %broadcast_in_dim.13), calls=%async_computation.4 | async-start | bytes 262144 | tf_op jit(solution)/shard_map/all_to_all | solution.py:64
  156.2 10.6 %copy-start.1 = (bf16[256,2048]{1,0:T(8,128)(2,1)S(1)}, bf16[256,2048]{1,0:T(8,128)(2,1)}, u32[]{:S(2)}) copy-start(bf16[256,2048]{1,0:T(8,128)(2,1)} %copy-done) | copy-start | bytes 3145732
  163.1 32.8 %all-to-all-start.3 = ((bf16[8,32,2048]{2,1,0:T(8,128)(2,1)}), bf16[8,32,2048]{2,1,0:T(8,128)(2,1)S(1)}, u32[]{:S(2)}, u32[]{:S(2)}) async-start(bf16[8,32,2048]{2,1,0:T(8,128)(2,1)} %fusion.2), calls=%async_computation.3 | async-start | bytes 2097152 | tf_op jit(solution)/shard_map/all_to_all | solution.py:151
  168.8 27.8 %collective-permute-start.8 = (bf16[1024,896]{1,0:T(8,128)(2,1)}, bf16[1024,896]{1,0:T(8,128)(2,1)}, u32[]{:S(2)}, u32[]{:S(2)}) collective-permute-start(bf16[1024,896]{1,0:T(8,128)(2,1)} %convolution_convert_fusion), channel_id=1, source_target_pairs={{0,1},{1,0},{2,3},{3,2},{4,5},{5,4},{6,7},{7,6},{8,9},{9,8},{10,11... | collective-permute-start | bytes 5505032 | tf_op jit(solution)/shard_map/ppermute | solution.py:55
  200.0 31.3 %all-to-all-start.6 = ((bf16[16,64,896]{2,1,0:T(8,128)(2,1)}), bf16[16,64,896]{2,1,0:T(8,128)(2,1)S(1)}, u32[]{:S(2)}, u32[]{:S(2)}) async-start(bf16[16,64,896]{2,1,0:T(8,128)(2,1)} %bitcast.31), calls=%async_computation.6 | async-start | bytes 3670016 | tf_op jit(solution)/shard_map/all_to_all | solution.py:138
  205.6 40.9 %collective-permute-start.7 = (bf16[32,2048]{1,0:T(8,128)(2,1)S(1)}, bf16[32,2048]{1,0:T(8,128)(2,1)S(1)}, u32[]{:S(2)}, u32[]{:S(2)}) collective-permute-start(bf16[32,2048]{1,0:T(8,128)(2,1)S(1)} %constant_dynamic-update-slice_fusion.20), channel_id=1, source_target_pairs={{0,0},{8,1},{16,2},{24,3},{32,4},{40,5},{48,6},{56,7},{4,8},{12,9}... | collective-permute-start | bytes 393224 | tf_op jit(solution)/shard_map/ppermute | solution.py:51
  232.1 13.7 %all-to-all-start.5 = ((f32[16,1,2048]{2,1,0:T(1,128)}), f32[16,1,2048]{2,1,0:T(1,128)S(1)}, u32[]{:S(2)}, u32[]{:S(2)}) async-start(f32[16,1,2048]{2,1,0:T(1,128)} %broadcast_in_dim.14), calls=%async_computation.5 | async-start | bytes 262144 | tf_op jit(solution)/shard_map/all_to_all | solution.py:64
  238.6 7.9 %collective-permute-start.9 = (bf16[32,896]{1,0:T(8,128)(2,1)S(1)}, bf16[32,896]{1,0:T(8,128)(2,1)S(1)}, u32[]{:S(2)}, u32[]{:S(2)}) collective-permute-start(bf16[32,896]{1,0:T(8,128)(2,1)S(1)} %get-tuple-element.33), channel_id=1, source_target_pairs={{8,0},{24,1},{40,2},{56,3},{0,4},{16,5},{32,6},{48,7},{12,8},{28,9... | collective-permute-start | bytes 172040 | tf_op jit(solution)/shard_map/ppermute | solution.py:51
  243.1 6.5 %collective-permute-start.10 = (bf16[32,896]{1,0:T(8,128)(2,1)S(1)}, bf16[32,896]{1,0:T(8,128)(2,1)S(1)}, u32[]{:S(2)}, u32[]{:S(2)}) collective-permute-start(bf16[32,896]{1,0:T(8,128)(2,1)S(1)} %get-tuple-element.34), channel_id=1, source_target_pairs={{0,0},{16,1},{32,2},{48,3},{8,4},{24,5},{40,6},{56,7},{4,8},{20,9}... | collective-permute-start | bytes 172040 | tf_op jit(solution)/shard_map/ppermute | solution.py:51
